TPU v7x, 32 devices: a whole 2x2x4 slice. The times are simulated.
32 devices in a mesh: peer: 8 (over y, x, core), zero: 4 (over z).
Axes of the slice: x: 2, y: 2, z: 4, core: 2. Of those that a mesh axis runs over, the one named last changes fastest.
Arguments:
- tokens: bfloat16 [8, 2048, 1024], P('peer', 'zero'), may hold values from -6 to 6
- out_grad: bfloat16 [8, 2048, 1024], P('peer', 'zero'), may hold values from -6 to 6
- step: int32 [1], replicated, may hold values from 0 to 3999
- up_param: float32 [8, 1024, 2048], P('peer', 'zero'), may hold values from -0.2 to 0.2
- down_param: float32 [8, 2048, 1024], P('peer', 'zero'), may hold values from -0.2 to 0.2
- up_first: float32 [8, 1024, 2048], P('peer', 'zero'), may hold values from -27.1529 to 27.1529
- down_first: float32 [8, 2048, 1024], P('peer', 'zero'), may hold values from -27.1529 to 27.1529
- up_second: float32 [8, 1024, 2048], P('peer', 'zero'), may hold values from 0.8192 to 819.2
- down_second: float32 [8, 2048, 1024], P('peer', 'zero'), may hold values from 0.8192 to 819.2
Outputs:
- new_up: float32 [8, 1024, 2048], P('peer', 'zero')
- new_down: float32 [8, 2048, 1024], P('peer', 'zero')
- new_up_first: float32 [8, 1024, 2048], P('peer', 'zero')
- new_down_first: float32 [8, 2048, 1024], P('peer', 'zero')
- new_up_second: float32 [8, 1024, 2048], P('peer', 'zero')
- new_down_second: float32 [8, 2048, 1024], P('peer', 'zero')
All inputs are finite; a program needn't handle non-finite values.
Results may differ from a plain program's by a relative error of at most 0.0065.
Values may be sent and summed in bfloat16 or wider, within the bound.
A program may use at most 128 MiB of HBM per device.

v0:
```python
from functools import partial
import jax
import jax.numpy as jnp
from jax import lax
from jax.sharding import PartitionSpec as P


def passed_along(array, axis, by):
    size = lax.axis_size(axis)
    return lax.ppermute(array, axis, [(i, (i + by) % size) for i in range(size)])


def gelu_tanh(values):
    return (
        0.5
        * values
        * (1.0 + jnp.tanh(0.7978845608 * (values + 0.044715 * values * values * values)))
    )


def adam_update(param, first, second, grad, first_fix, second_fix):
    first_new = 0.9 * first + 0.1 * grad
    second_new = 0.999 * second + 0.001 * grad * grad
    local = param - 0.01 * (first_new / first_fix) / (jnp.sqrt(second_new / second_fix) + 1e-08)
    return (local, first_new, second_new)


def across_rows(left, right):
    return lax.dot_general(
        left, right, (((0,), (0,)), ((), ())), preferred_element_type=jnp.float32
    )


def from_partner(pair, by):
    return passed_along(pair, "peer", -by)


def body(
    tokens, out_grad, step, up_param, down_param, up_first, down_first, up_second, down_second
):
    grad_rows = out_grad[0]
    widened = tokens[0].astype(jnp.float32)
    center = jnp.mean(widened, axis=1, keepdims=True)
    spread = jnp.mean((widened - center) * (widened - center), axis=1, keepdims=True)
    normed = ((widened - center) * lax.rsqrt(spread + 1e-05)).astype(jnp.bfloat16)
    up_low = up_param[0].astype(jnp.bfloat16)
    down_low = down_param[0].astype(jnp.bfloat16)
    columns = normed
    pre = jnp.dot(
        columns,
        lax.all_gather(up_low, "zero", axis=0, tiled=True),
        preferred_element_type=jnp.float32,
    )
    active, backward = jax.vjp(gelu_tanh, pre)
    act_grad = lax.dot_general(
        grad_rows,
        lax.all_gather(down_low, "zero", axis=0, tiled=True),
        (((1,), (1,)), ((), ())),
        preferred_element_type=jnp.float32,
    )
    act = active.astype(jnp.bfloat16)
    pre_grad = backward(act_grad)[0].astype(jnp.bfloat16)
    columns = normed
    up_grad = lax.psum_scatter(
        across_rows(columns, pre_grad).astype(jnp.bfloat16), "zero", scatter_dimension=0, tiled=True
    ).astype(jnp.float32)
    columns = act
    down_grad = lax.psum_scatter(
        across_rows(columns, grad_rows).astype(jnp.bfloat16),
        "zero",
        scatter_dimension=0,
        tiled=True,
    ).astype(jnp.float32)
    count = (step[0] + 1).astype(jnp.float32)
    first_fix = 1.0 - jnp.power(jnp.float32(0.9), count)
    second_fix = 1.0 - jnp.power(jnp.float32(0.999), count)
    up_local, up_first_new, up_second_new = adam_update(
        up_param[0], up_first[0], up_second[0], up_grad, first_fix, second_fix
    )
    down_local, down_first_new, down_second_new = adam_update(
        down_param[0], down_first[0], down_second[0], down_grad, first_fix, second_fix
    )
    levels = lax.axis_size("peer").bit_length() - 1
    branches = [partial(from_partner, by=2**level) for level in range(levels)]
    up_other, down_other = lax.switch(step[0] % levels, branches, (up_local, down_local))
    new_up = 0.5 * (up_local + up_other)
    new_down = 0.5 * (down_local + down_other)
    return (
        new_up[None],
        new_down[None],
        up_first_new[None],
        down_first_new[None],
        up_second_new[None],
        down_second_new[None],
    )


def solution(mesh):
    in_specs = (
        P("peer", "zero", None),
        P("peer", "zero", None),
        P(),
        P("peer", "zero", None),
        P("peer", "zero", None),
        P("peer", "zero", None),
        P("peer", "zero", None),
        P("peer", "zero", None),
        P("peer", "zero", None),
    )
    out_specs = (
        P("peer", "zero", None),
        P("peer", "zero", None),
        P("peer", "zero", None),
        P("peer", "zero", None),
        P("peer", "zero", None),
        P("peer", "zero", None),
    )
    return jax.shard_map(body, mesh=mesh, in_specs=in_specs, out_specs=out_specs, check_vma=False)
```

profile of v0, /device:TPU:0, one launch (start us, length us, event | category | flops | bytes accessed | tf_op | source)
XLA Modules:
  0.0 454.6 jit_solution(11228907826659699742)
XLA Ops:
  7.2 0.0 copy-start
  7.2 0.0 copy-start.1
  7.2 0.0 all-gather.3.cloned.1.call-start
  7.2 2.9 bitcast_convert_fusion.1
  10.1 0.0 all-gather.3.cloned.1.call-update
  10.1 0.0 all-gather.5.cloned.1.call-start
  10.2 0.0 copy-done.1
  10.2 1.1 bitcast_convert_fusion
  11.3 0.0 copy-start.2
  11.3 0.0 all-gather.5.cloned.1.call-update
  11.3 0.0 reduce-scatter.3.cloned.1.call-start
  11.4 1.5 convert_reduce_fusion
  12.9 0.0 copy-done.2
  12.9 0.4 fusion.9
  13.3 80.4 %all-gather.3.cloned.1.call-done = bf16[1024,2048]{1,0:T(8,128)(2,1)} async-done(((bf16[256,2048]{1,0:T(8,128)(2,1)}), bf16[1024,2048]{1,0:T(8,128)(2,1)}) %all-gather.3.cloned.1.call-update) | async-done | bytes 4194320 | tf_op jit(solution)/shard_map/all_gather | solution.py:51
  93.7 6.6 %fusion.40 = f32[512,2048]{1,0:T(8,128)} fusion(bf16[1024,2048]{1,0:T(8,128)(2,1)} %all-gather.3.cloned.1.call-done, bf16[1,512,1024]{2,1,0:T(8,128)(2,1)S(1)} %copy-done.2, f32[512]{0:T(512)S(1)} %add_rsqrt_fusion, f32[512]{0:T(512)S(1)} %broadcast_multiply_fusion), kind=kOutput, calls=%fused_computation.55 | convolution fusion | flops 2149580800 | bytes 9441280 | tf_op jit(solution)/shard_map/dot_general | solution.py:49
  100.3 74.8 %all-gather.5.cloned.1.call-done = bf16[2048,1024]{1,0:T(8,128)(2,1)} async-done(((bf16[512,1024]{1,0:T(8,128)(2,1)}), bf16[2048,1024]{1,0:T(8,128)(2,1)}) %all-gather.5.cloned.1.call-update) | async-done | bytes 4194320 | tf_op jit(solution)/shard_map/all_gather | solution.py:57
  175.1 0.0 copy-done
  175.1 11.0 %convolution_convert_fusion.1 = bf16[1024,2048]{1,0:T(8,128)(2,1)} fusion(f32[512,2048]{1,0:T(8,128)} %fusion.40, bf16[2048,1024]{1,0:T(8,128)(2,1)} %all-gather.5.cloned.1.call-done, bf16[1,512,1024]{2,1,0:T(8,128)(2,1)S(1)} %copy-done, bf16[1,512,1024]{2,1,0:T(8,128)(2,1)S(1)} %copy-done.2, f32[512]{0:T(512)S(1)} %add_rsqrt_fusion, ...), kind=kOutput, calls=%fused_computation.12 | convolution fusion | flops 4324327424 | bytes 14684160 | tf_op jit(solution)/shard_map/dot_general | solution.py:29
  186.2 0.0 reduce-scatter.3.cloned.1.call-update
  186.2 0.2 reduce-scatter.5.cloned.1.call-start
  186.4 7.1 %convolution_convert_fusion = bf16[2048,1024]{1,0:T(8,128)(2,1)} fusion(f32[512,2048]{1,0:T(8,128)} %fusion.40, bf16[1,512,1024]{2,1,0:T(8,128)(2,1)S(1)} %copy-done), kind=kOutput, calls=%fused_computation.11 | convolution fusion | flops 2159017984 | bytes 9437184 | tf_op jit(solution)/shard_map/dot_general | solution.py:29
  193.5 0.0 reduce-scatter.5.cloned.1.call-update
  194.3 67.3 %reduce-scatter.3.cloned.1.call-done = bf16[256,2048]{1,0:T(8,128)(2,1)} async-done(((bf16[1024,2048]{1,0:T(8,128)(2,1)}), bf16[256,2048]{1,0:T(8,128)(2,1)}) %reduce-scatter.3.cloned.1.call-update) | async-done | bytes 1048592 | tf_op jit(solution)/shard_map/reduce_scatter | solution.py:64
  261.6 6.7 %fusion.23 = (f32[1,256,2048]{2,1,0:T(8,128)}, f32[256,2048]{1,0:T(8,128)S(1)}, f32[1,256,2048]{2,1,0:T(8,128)}) fusion(bf16[256,2048]{1,0:T(8,128)(2,1)} %reduce-scatter.3.cloned.1.call-done, f32[1,256,2048]{2,1,0:T(8,128)} %param.19, f32[]{:T(128)} %bitcast.7, f32[]{:T(128)} %bitcast.5, f32[1,256,2048]{2,1,0:T(8,128)} %param.17, f32[1,256,2048]{2,1,0:T(8,128)} %param.15), kind=kLoop, calls=%fused_computation.41 | loop fusion | flops 7340032 | bytes 13631496 | tf_op jit(solution)/shard_map/broadcast_in_dim | solution.py:93
  268.3 72.8 %reduce-scatter.5.cloned.1.call-done = bf16[512,1024]{1,0:T(8,128)(2,1)} async-done(((bf16[2048,1024]{1,0:T(8,128)(2,1)}), bf16[512,1024]{1,0:T(8,128)(2,1)}) %reduce-scatter.5.cloned.1.call-update) | async-done | bytes 1048592 | tf_op jit(solution)/shard_map/reduce_scatter | solution.py:68
  341.1 7.5 %fusion.22 = (f32[1,512,1024]{2,1,0:T(8,128)}, f32[512,1024]{1,0:T(8,128)}, f32[1,512,1024]{2,1,0:T(8,128)}) fusion(bf16[512,1024]{1,0:T(8,128)(2,1)} %reduce-scatter.5.cloned.1.call-done, f32[1,512,1024]{2,1,0:T(8,128)} %param.20, f32[]{:T(128)} %bitcast.7, f32[]{:T(128)} %bitcast.5, f32[1,512,1024]{2,1,0:T(8,128)} %param.18, f32[1,512,1024]{2,1,0:T(8,128)} %param.16), kind=kLoop, calls=%fused_computation.40 | loop fusion | flops 7340032 | bytes 13631496 | tf_op jit(solution)/shard_map/broadcast_in_dim | solution.py:94
  348.6 92.1 %conditional.1 = (f32[256,2048]{1,0:T(8,128)}, f32[512,1024]{1,0:T(8,128)}) conditional(s32[]{:T(128)} %clamp.3, (f32[256,2048]{1,0:T(8,128)S(1)}, f32[512,1024]{1,0:T(8,128)}) %tuple.20, (f32[256,2048]{1,0:T(8,128)S(1)}, f32[512,1024]{1,0:T(8,128)}) %tuple.20, (f32[256,2048]{1,0:T(8,128)S(1)}, f32[512,1024]{1,0:T(8,128)}) %tuple.20), branch_computations={%region_4.5_spmd, %region_5.6_spmd, %region_6.7_spmd} | conditional | bytes 16777312 | solution.py:85
  348.6 2.4 collective-permute-start.2
  351.0 0.6 collective-permute-start.3
  351.5 45.7 %collective-permute-done.2 = f32[256,2048]{1,0:T(8,128)} collective-permute-done((f32[256,2048]{1,0:T(8,128)S(1)}, f32[256,2048]{1,0:T(8,128)}, u32[]{:S(2)}, u32[]{:S(2)}) %collective-permute-start.2) | collective-permute-done | bytes 2097184 | tf_op jit(solution)/shard_map/cond/branch_1_fun/ppermute | solution.py:10
  397.2 43.5 %collective-permute-done.3 = f32[512,1024]{1,0:T(8,128)} collective-permute-done((f32[512,1024]{1,0:T(8,128)}, f32[512,1024]{1,0:T(8,128)}, u32[]{:S(2)}, u32[]{:S(2)}) %collective-permute-start.3) | collective-permute-done | bytes 2097184 | tf_op jit(solution)/shard_map/cond/branch_1_fun/ppermute | solution.py:10
  440.7 3.2 multiply_bitcast_fusion.1
  443.9 4.2 multiply_bitcast_fusion
  (2 shorter events, 0.0 us)
Async XLA Ops:
  7.2 168.0 %copy-start = (bf16[1,512,1024]{2,1,0:T(8,128)(2,1)S(1)}, bf16[1,512,1024]{2,1,0:T(8,128)(2,1)}, u32[]{:S(2)}) copy-start(bf16[1,512,1024]{2,1,0:T(8,128)(2,1)} %param.13) | copy-start | bytes 3145732
  7.2 3.0 copy-start.1
  7.2 86.6 %all-gather.3.cloned.1.call-start = ((), (), s32[]{:S(2)}) async-start(), calls=%async_computation.2 | async-start | bytes 5242880 | tf_op jit(solution)/shard_map/all_gather | solution.py:51
  10.1 165.0 %all-gather.5.cloned.1.call-start = ((), (), s32[]{:S(2)}) async-start(), calls=%async_computation.3 | async-start | bytes 5242880 | tf_op jit(solution)/shard_map/all_gather | solution.py:57
  11.3 1.6 copy-start.2
  11.3 250.3 %reduce-scatter.3.cloned.1.call-start = ((), (), s32[]{:S(2)}) async-start(), calls=%async_computation.4 | async-start | bytes 5242880 | tf_op jit(solution)/shard_map/reduce_scatter | solution.py:64
  186.2 154.9 %reduce-scatter.5.cloned.1.call-start = ((), (), s32[]{:S(2)}) async-start(), calls=%async_computation.5 | async-start | bytes 5242880 | tf_op jit(solution)/shard_map/reduce_scatter | solution.py:68
  348.6 48.6 %collective-permute-start.2 = (f32[256,2048]{1,0:T(8,128)S(1)}, f32[256,2048]{1,0:T(8,128)}, u32[]{:S(2)}, u32[]{:S(2)}) collective-permute-start(f32[256,2048]{1,0:T(8,128)S(1)} %get-tuple-element.14), channel_id=1, source_target_pairs={{0,24},{4,28},{8,0},{12,4},{16,8},{20,12},{24,16},{28,20},{1,25},{... | collective-permute-start | bytes 6291464 | tf_op jit(solution)/shard_map/cond/branch_1_fun/ppermute | solution.py:10
  351.0 89.7 %collective-permute-start.3 = (f32[512,1024]{1,0:T(8,128)}, f32[512,1024]{1,0:T(8,128)}, u32[]{:S(2)}, u32[]{:S(2)}) collective-permute-start(f32[512,1024]{1,0:T(8,128)} %get-tuple-element.15), channel_id=1, source_target_pairs={{0,24},{4,28},{8,0},{12,4},{16,8},{20,12},{24,16},{28,20},{1,25},{... | collective-permute-start | bytes 6291464 | tf_op jit(solution)/shard_map/cond/branch_1_fun/ppermute | solution.py:10
Sparse Core Ops, SparseCore 0:
  10.2 83.4 all-gather.2
  95.9 79.2 all-gather.4
  186.3 75.2 reduce-scatter.2
  263.8 77.2 reduce-scatter.4
where the time goes:
time: 455 us
  waiting for transfers between devices  385 us (85%)
  other arithmetic  27.5 us (6%)
  matrix products  24.7 us (5%)
  between operations  14.5 us (3%)
    ppermute x2, waiting for transfers between devices, passed_along(): lax.ppermute(array, axis, [(i, (i + by) % size) for i in range(size)])  89.2 us
    all_gather x1, waiting for transfers between devices, body(): lax.all_gather(up_low, 'zero', axis=0, tiled=True)  80.4 us
    all_gather x1, waiting for transfers between devices, body(): lax.all_gather(down_low, 'zero', axis=0, tiled=True)  74.8 us
    reduce_scatter x1, waiting for transfers between devices, body(): lax.psum_scatter(across_rows(columns, grad_rows).astype(jnp.bfloat16), 'z...  72.8 us
    reduce_scatter x1, waiting for transfers between devices, body(): lax.psum_scatter(across_rows(columns, pre_grad).astype(jnp.bfloat16), 'ze...  67.3 us
    dot_general x2, matrix products, across_rows(): lax.dot_general(left, right, (((0,), (0,)), ((), ())), preferred_element_...  18.1 us
  transfers between devices with their start and end apart: 6, of which 6 were waited for; matrix products, arithmetic and copies ran while one was open for 5% of the time, Pallas kernels for 0%

commit v1 on v0

--- a/solution.py
+++ b/solution.py
@@ -3,6 +3,23 @@
 import jax.numpy as jnp
 from jax import lax
 from jax.sharding import PartitionSpec as P
+
+
+def in_order(blocks, dim):
+    blocks = jnp.moveaxis(blocks, 0, dim)
+    shape = blocks.shape
+    return blocks.reshape(*shape[:dim], shape[dim] * shape[dim + 1], *shape[dim + 2 :])
+
+
+def collect(array, axis, dim):
+    size = lax.axis_size(axis)
+    right = [(i, (i + 1) % size) for i in range(size)]
+    blocks = [array]
+    while len(blocks) < size:
+        blocks.append(lax.ppermute(blocks[-1], axis, right))
+    mine = lax.axis_index(axis)
+    blocks = jnp.stack(blocks)[(mine - jnp.arange(size)) % size]
+    return in_order(blocks, dim)
 
 
 def passed_along(array, axis, by):
@@ -46,11 +63,7 @@
     up_low = up_param[0].astype(jnp.bfloat16)
     down_low = down_param[0].astype(jnp.bfloat16)
     columns = normed
-    pre = jnp.dot(
-        columns,
-        lax.all_gather(up_low, "zero", axis=0, tiled=True),
-        preferred_element_type=jnp.float32,
-    )
+    pre = jnp.dot(columns, collect(up_low, "zero", 0), preferred_element_type=jnp.float32)
     active, backward = jax.vjp(gelu_tanh, pre)
     act_grad = lax.dot_general(
         grad_rows,

time: 455 us -> 444 us (0.976)
  waiting for transfers between devices: 385 us -> 336 us
  starting transfers between devices: 3.29 us -> 33.3 us
  local copies, waits for them, and re-layouts: 0.02 us -> 7.01 us
  other arithmetic: 27.5 us -> 32.1 us
    ppermute x0 -> x3, waiting for transfers between devices: none -> 109 us  [collect(): blocks.append(lax.ppermute(blocks[-1], axis, right))]
    all_gather x1 -> x0, waiting for transfers between devices: 80.4 us -> none  [body(): lax.all_gather(up_low, 'zero', axis=0, tiled=True)]
    all_gather x1, waiting for transfers between devices: 74.8 us -> 0.02 us  [body(): lax.all_gather(down_low, 'zero', axis=0, tiled=True)]
    ppermute x0 -> x3, starting transfers between devices: none -> 30 us  [collect(): blocks.append(lax.ppermute(blocks[-1], axis, right))]
    reduce_scatter x1, waiting for transfers between devices: 72.8 us -> 64.2 us  [body(): lax.psum_scatter(across_rows(columns, grad_rows).astype(jnp.bfloat16), 'z...]
    reduce_scatter x1, waiting for transfers between devices: 67.3 us -> 72.9 us  [body(): lax.psum_scatter(across_rows(columns, pre_grad).astype(jnp.bfloat16), 'ze...]
    gather x0 -> x1, local copies, waits for them, and re-layouts: none -> 5.06 us  [collect(): blocks = jnp.stack(blocks)[(mine - jnp.arange(size)) % size]]
  transfers between devices with their start and end apart: 6 -> 8, of which waited for: 6 -> 7; matrix products, arithmetic and copies ran while one was open for 5% -> 9% of each run, Pallas kernels for 0% -> 0%
where the time goes in v1:
time: 444 us
  waiting for transfers between devices  336 us (76%)
  starting transfers between devices  33.3 us (7%)
  other arithmetic  32.1 us (7%)
  matrix products  20.6 us (5%)
  between operations  14.6 us (3%)
  local copies, waits for them, and re-layouts  7.01 us (2%)
    ppermute x3, waiting for transfers between devices, collect(): blocks.append(lax.ppermute(blocks[-1], axis, right))  109 us
    ppermute x2, waiting for transfers between devices, passed_along(): lax.ppermute(array, axis, [(i, (i + by) % size) for i in range(size)])  89.4 us
    reduce_scatter x1, waiting for transfers between devices, body(): lax.psum_scatter(across_rows(columns, pre_grad).astype(jnp.bfloat16), 'ze...  72.9 us
    reduce_scatter x1, waiting for transfers between devices, body(): lax.psum_scatter(across_rows(columns, grad_rows).astype(jnp.bfloat16), 'z...  64.2 us
    ppermute x3, starting transfers between devices, collect(): blocks.append(lax.ppermute(blocks[-1], axis, right))  30 us
    dot_general x2, matrix products, across_rows(): lax.dot_general(left, right, (((0,), (0,)), ((), ())), preferred_element_...  16 us
  transfers between devices with their start and end apart: 8, of which 7 were waited for; matrix products, arithmetic and copies ran while one was open for 9% of the time, Pallas kernels for 0%

profile of v1, /device:TPU:0, one launch (start us, length us, event | category | flops | bytes accessed | tf_op | source)
XLA Modules:
  0.0 443.6 jit_solution(2718070982692196620)
XLA Ops:
  7.2 0.0 copy-start
  7.2 0.0 copy-start.2
  7.2 0.0 all-gather.2.cloned.1.call-start
  7.2 2.9 bitcast_convert_fusion
  10.1 0.0 all-gather.2.cloned.1.call-update
  10.1 0.0 reduce-scatter.5.cloned.1.call-start
  10.2 0.0 copy-done.2
  10.2 1.1 fusion.51
  11.3 0.0 copy-start.4
  11.4 3.1 collective-permute-start.6
  14.4 39.8 %collective-permute-done.6 = bf16[256,2048]{1,0:T(8,128)(2,1)S(1)} collective-permute-done((bf16[256,2048]{1,0:T(8,128)(2,1)S(1)}, bf16[256,2048]{1,0:T(8,128)(2,1)S(1)}, u32[]{:S(2)}, u32[]{:S(2)}) %collective-permute-start.6) | collective-permute-done | bytes 1048608 | tf_op jit(solution)/shard_map/ppermute | solution.py:19
  54.2 16.7 %collective-permute-start.7 = (bf16[256,2048]{1,0:T(8,128)(2,1)S(1)}, bf16[256,2048]{1,0:T(8,128)(2,1)}, u32[]{:S(2)}, u32[]{:S(2)}) collective-permute-start(bf16[256,2048]{1,0:T(8,128)(2,1)S(1)} %collective-permute-done.6), channel_id=1, source_target_pairs={{0,1},{1,2},{2,3},{3,0},{4,5},{5,6},{6,7},{7,4},{8,9},{9,10},{10,1... | collective-permute-start | bytes 3145736 | tf_op jit(solution)/shard_map/ppermute | solution.py:19
  70.9 47.1 %collective-permute-done.7 = bf16[256,2048]{1,0:T(8,128)(2,1)} collective-permute-done((bf16[256,2048]{1,0:T(8,128)(2,1)S(1)}, bf16[256,2048]{1,0:T(8,128)(2,1)}, u32[]{:S(2)}, u32[]{:S(2)}) %collective-permute-start.7) | collective-permute-done | bytes 1048608 | tf_op jit(solution)/shard_map/ppermute | solution.py:19
  118.0 10.3 %collective-permute-start.8 = (bf16[256,2048]{1,0:T(8,128)(2,1)}, bf16[256,2048]{1,0:T(8,128)(2,1)}, u32[]{:S(2)}, u32[]{:S(2)}) collective-permute-start(bf16[256,2048]{1,0:T(8,128)(2,1)} %collective-permute-done.7), channel_id=1, source_target_pairs={{0,1},{1,2},{2,3},{3,0},{4,5},{5,6},{6,7},{7,4},{8,9},{9,10},{10,1... | collective-permute-start | bytes 3145736 | tf_op jit(solution)/shard_map/ppermute | solution.py:19
  128.3 1.4 convert_reduce_fusion
  129.8 1.6 fusion.11
  131.4 22.5 %collective-permute-done.8 = bf16[256,2048]{1,0:T(8,128)(2,1)} collective-permute-done((bf16[256,2048]{1,0:T(8,128)(2,1)}, bf16[256,2048]{1,0:T(8,128)(2,1)}, u32[]{:S(2)}, u32[]{:S(2)}) %collective-permute-start.8) | collective-permute-done | bytes 1048608 | tf_op jit(solution)/shard_map/ppermute | solution.py:19
  153.9 0.0 copy-done.4
  153.9 3.4 pad_maximum_fusion
  157.4 0.0 copy-start.3
  157.4 5.1 %gather_fusion = bf16[4,256,2048]{2,1,0:T(8,128)(2,1)} fusion(bf16[4,256,2048]{2,1,0:T(8,128)(2,1)} %pad_maximum_fusion, s32[1024]{0:T(1024)S(1)} %pad_clamp_fusion), kind=kCustom, calls=%fused_computation | custom fusion | bytes 8388624 | tf_op jit(solution)/shard_map/gather | solution.py:21
  162.4 0.0 copy-done.3
  162.4 4.6 %fusion.27 = f32[512,2048]{1,0:T(8,128)S(1)} fusion(bf16[1024,2048]{1,0:T(8,128)(2,1)} %bitcast.78, bf16[1,512,1024]{2,1,0:T(8,128)(2,1)S(1)} %copy-done.3, f32[512]{0:T(512)S(1)} %add_rsqrt_fusion, f32[512]{0:T(512)S(1)} %broadcast_multiply_fusion), kind=kOutput, calls=%fused_computation.48 | convolution fusion | flops 2149580800 | bytes 9441280 | tf_op jit(solution)/shard_map/dot_general | solution.py:66
  167.0 0.0 copy-start.5
  167.1 1.9 copy-done.5
  169.0 0.0 copy-done
  169.0 4.9 %convolution_convert_fusion = bf16[2048,1024]{1,0:T(8,128)(2,1)} fusion(f32[512,2048]{1,0:T(8,128)S(1)} %fusion.27, bf16[1,512,1024]{2,1,0:T(8,128)(2,1)S(1)} %copy-done), kind=kOutput, calls=%fused_computation.13 | convolution fusion | flops 2159017984 | bytes 9437184 | tf_op jit(solution)/shard_map/dot_general | solution.py:46
  173.9 0.0 reduce-scatter.5.cloned.1.call-update
  174.0 0.2 reduce-scatter.3.cloned.1.call-start
  174.2 0.0 all-gather.2.cloned.1.call-done
  174.2 11.1 %convolution_convert_fusion.1 = bf16[1024,2048]{1,0:T(8,128)(2,1)} fusion(f32[512,2048]{1,0:T(8,128)} %copy-done.5, bf16[1,512,1024]{2,1,0:T(8,128)(2,1)S(1)} %copy-done.3, bf16[2048,1024]{1,0:T(8,128)(2,1)} %all-gather.2.cloned.1.call-done, bf16[1,512,1024]{2,1,0:T(8,128)(2,1)S(1)} %copy-done, f32[512]{0:T(512)S(1)} %add_rsqrt_fusion, ...), kind=kOutput, calls=%fused_computation.14 | convolution fusion | flops 4324327424 | bytes 14684160 | tf_op jit(solution)/shard_map/dot_general | solution.py:46
  185.3 0.0 reduce-scatter.3.cloned.1.call-update
  186.1 64.2 %reduce-scatter.5.cloned.1.call-done = bf16[512,1024]{1,0:T(8,128)(2,1)} async-done(((bf16[2048,1024]{1,0:T(8,128)(2,1)}), bf16[512,1024]{1,0:T(8,128)(2,1)}) %reduce-scatter.5.cloned.1.call-update) | async-done | bytes 1048592 | tf_op jit(solution)/shard_map/reduce_scatter | solution.py:81
  250.3 6.7 %fusion.24 = (f32[1,512,1024]{2,1,0:T(8,128)}, f32[512,1024]{1,0:T(8,128)S(1)}, f32[1,512,1024]{2,1,0:T(8,128)}) fusion(bf16[512,1024]{1,0:T(8,128)(2,1)} %reduce-scatter.5.cloned.1.call-done, f32[1,512,1024]{2,1,0:T(8,128)} %param.20, f32[]{:T(128)} %bitcast.13, f32[]{:T(128)} %bitcast.11, f32[1,512,1024]{2,1,0:T(8,128)} %param.18, f32[1,512,1024]{2,1,0:T(8,128)} %param.16), kind=kLoop, calls=%fused_computation.45 | loop fusion | flops 7340032 | bytes 13631496 | tf_op jit(solution)/shard_map/broadcast_in_dim | solution.py:107
  257.0 72.9 %reduce-scatter.3.cloned.1.call-done = bf16[256,2048]{1,0:T(8,128)(2,1)} async-done(((bf16[1024,2048]{1,0:T(8,128)(2,1)}), bf16[256,2048]{1,0:T(8,128)(2,1)}) %reduce-scatter.3.cloned.1.call-update) | async-done | bytes 1048592 | tf_op jit(solution)/shard_map/reduce_scatter | solution.py:77
  329.9 7.4 %fusion.25 = (f32[1,256,2048]{2,1,0:T(8,128)}, f32[256,2048]{1,0:T(8,128)}, f32[1,256,2048]{2,1,0:T(8,128)}) fusion(bf16[256,2048]{1,0:T(8,128)(2,1)} %reduce-scatter.3.cloned.1.call-done, f32[1,256,2048]{2,1,0:T(8,128)} %param.19, f32[]{:T(128)} %bitcast.13, f32[]{:T(128)} %bitcast.11, f32[1,256,2048]{2,1,0:T(8,128)} %param.17, f32[1,256,2048]{2,1,0:T(8,128)} %param.15), kind=kLoop, calls=%fused_computation.46 | loop fusion | flops 7340032 | bytes 13631496 | tf_op jit(solution)/shard_map/broadcast_in_dim | solution.py:106
  337.4 92.3 %conditional.1 = (f32[256,2048]{1,0:T(8,128)}, f32[512,1024]{1,0:T(8,128)}) conditional(s32[]{:T(128)} %clamp.3, (f32[256,2048]{1,0:T(8,128)}, f32[512,1024]{1,0:T(8,128)S(1)}) %tuple.20, (f32[256,2048]{1,0:T(8,128)}, f32[512,1024]{1,0:T(8,128)S(1)}) %tuple.20, (f32[256,2048]{1,0:T(8,128)}, f32[512,1024]{1,0:T(8,128)S(1)}) %tuple.20), branch_computations={%region_4.5_spmd, %region_5.6_spmd, %region_6.7_spmd} | conditional | bytes 16777312 | solution.py:98
  337.4 2.4 collective-permute-start.2
  339.8 0.6 collective-permute-start.3
  340.3 45.9 %collective-permute-done.2 = f32[256,2048]{1,0:T(8,128)} collective-permute-done((f32[256,2048]{1,0:T(8,128)}, f32[256,2048]{1,0:T(8,128)}, u32[]{:S(2)}, u32[]{:S(2)}) %collective-permute-start.2) | collective-permute-done | bytes 2097184 | tf_op jit(solution)/shard_map/cond/branch_1_fun/ppermute | solution.py:27
  386.2 43.5 %collective-permute-done.3 = f32[512,1024]{1,0:T(8,128)} collective-permute-done((f32[512,1024]{1,0:T(8,128)S(1)}, f32[512,1024]{1,0:T(8,128)}, u32[]{:S(2)}, u32[]{:S(2)}) %collective-permute-start.3) | collective-permute-done | bytes 2097184 | tf_op jit(solution)/shard_map/cond/branch_1_fun/ppermute | solution.py:27
  429.7 4.0 multiply_bitcast_fusion.1
  433.7 0.0 copy-start.1
  433.7 3.4 multiply_bitcast_fusion
  437.1 0.0 copy-done.1
  (4 shorter events, 0.0 us)
Async XLA Ops:
  7.2 161.8 %copy-start = (bf16[1,512,1024]{2,1,0:T(8,128)(2,1)S(1)}, bf16[1,512,1024]{2,1,0:T(8,128)(2,1)}, u32[]{:S(2)}) copy-start(bf16[1,512,1024]{2,1,0:T(8,128)(2,1)} %param.13) | copy-start | bytes 3145732
  7.2 3.0 copy-start.2
  7.2 167.0 %all-gather.2.cloned.1.call-start = ((), (), s32[]{:S(2)}) async-start(), calls=%async_computation.2 | async-start | bytes 5242880 | tf_op jit(solution)/shard_map/all_gather | solution.py:70
  10.1 240.1 %reduce-scatter.5.cloned.1.call-start = ((), (), s32[]{:S(2)}) async-start(), calls=%async_computation.4 | async-start | bytes 5242880 | tf_op jit(solution)/shard_map/reduce_scatter | solution.py:81
  11.3 142.6 %copy-start.4 = (bf16[1,256,2048]{2,1,0:T(8,128)(2,1)S(1)}, bf16[1,256,2048]{2,1,0:T(8,128)(2,1)}, u32[]{:S(2)}) copy-start(bf16[1,256,2048]{2,1,0:T(8,128)(2,1)} %get-tuple-element.34) | copy-start | bytes 3145732
  11.4 42.9 %collective-permute-start.6 = (bf16[256,2048]{1,0:T(8,128)(2,1)S(1)}, bf16[256,2048]{1,0:T(8,128)(2,1)S(1)}, u32[]{:S(2)}, u32[]{:S(2)}) collective-permute-start(bf16[256,2048]{1,0:T(8,128)(2,1)S(1)} %get-tuple-element.35), channel_id=1, source_target_pairs={{0,1},{1,2},{2,3},{3,0},{4,5},{5,6},{6,7},{7,4},{8,9},{9,10},{10,1... | collective-permute-start | bytes 3145736 | tf_op jit(solution)/shard_map/ppermute | solution.py:19
  54.2 63.7 %collective-permute-start.7 = (bf16[256,2048]{1,0:T(8,128)(2,1)S(1)}, bf16[256,2048]{1,0:T(8,128)(2,1)}, u32[]{:S(2)}, u32[]{:S(2)}) collective-permute-start(bf16[256,2048]{1,0:T(8,128)(2,1)S(1)} %collective-permute-done.6), channel_id=1, source_target_pairs={{0,1},{1,2},{2,3},{3,0},{4,5},{5,6},{6,7},{7,4},{8,9},{9,10},{10,1... | collective-permute-start | bytes 3145736 | tf_op jit(solution)/shard_map/ppermute | solution.py:19
  118.0 36.0 %collective-permute-start.8 = (bf16[256,2048]{1,0:T(8,128)(2,1)}, bf16[256,2048]{1,0:T(8,128)(2,1)}, u32[]{:S(2)}, u32[]{:S(2)}) collective-permute-start(bf16[256,2048]{1,0:T(8,128)(2,1)} %collective-permute-done.7), channel_id=1, source_target_pairs={{0,1},{1,2},{2,3},{3,0},{4,5},{5,6},{6,7},{7,4},{8,9},{9,10},{10,1... | collective-permute-start | bytes 3145736 | tf_op jit(solution)/shard_map/ppermute | solution.py:19
  157.4 5.1 %copy-start.3 = (bf16[1,512,1024]{2,1,0:T(8,128)(2,1)S(1)}, bf16[1,512,1024]{2,1,0:T(8,128)(2,1)}, u32[]{:S(2)}) copy-start(bf16[1,512,1024]{2,1,0:T(8,128)(2,1)} %param.12) | copy-start | bytes 3145732
  167.0 1.9 copy-start.5
  174.0 156.0 %reduce-scatter.3.cloned.1.call-start = ((), (), s32[]{:S(2)}) async-start(), calls=%async_computation.3 | async-start | bytes 5242880 | tf_op jit(solution)/shard_map/reduce_scatter | solution.py:77
  337.4 48.8 %collective-permute-start.2 = (f32[256,2048]{1,0:T(8,128)}, f32[256,2048]{1,0:T(8,128)}, u32[]{:S(2)}, u32[]{:S(2)}) collective-permute-start(f32[256,2048]{1,0:T(8,128)} %get-tuple-element.14), channel_id=1, source_target_pairs={{0,24},{4,28},{8,0},{12,4},{16,8},{20,12},{24,16},{28,20},{1,25},{... | collective-permute-start | bytes 6291464 | tf_op jit(solution)/shard_map/cond/branch_1_fun/ppermute | solution.py:27
  339.8 89.9 %collective-permute-start.3 = (f32[512,1024]{1,0:T(8,128)S(1)}, f32[512,1024]{1,0:T(8,128)}, u32[]{:S(2)}, u32[]{:S(2)}) collective-permute-start(f32[512,1024]{1,0:T(8,128)S(1)} %get-tuple-element.15), channel_id=1, source_target_pairs={{0,24},{4,28},{8,0},{12,4},{16,8},{20,12},{24,16},{28,20},{1,25},{... | collective-permute-start | bytes 6291464 | tf_op jit(solution)/shard_map/cond/branch_1_fun/ppermute | solution.py:27
  433.7 3.4 copy-start.1
Sparse Core Ops, SparseCore 0:
  10.3 119.7 all-gather.1
  174.1 76.1 reduce-scatter.4
  252.6 77.2 reduce-scatter.2
